TPU v7x, 32 devices: a whole 2x2x4 slice. The times are simulated.
32 devices in a mesh: win: 4 (over y, core), tile: 8 (over z, x).
Axes of the slice: x: 2, y: 2, z: 4, core: 2. Of those that a mesh axis runs over, the one named last changes fastest.
Arguments:
- state: float32 [4, 8, 5, 32, 8, 128], P('win', 'tile'), may hold values from -6 to 6
- obs_weight: float32 [4, 8, 5, 32, 8, 128], P('win', 'tile'), may hold values from 0 to 1
- trajectory: bfloat16 [4, 8, 3, 2, 32, 8, 128], P('win', 'tile'), may hold values from -0.8984375 to 0.8984375
- coupling: float32 [5, 5], replicated, may hold values from -0.9 to 0.9
- prec_scale: float32 [5, 32], replicated, may hold values from 0.5 to 2
Outputs:
- hess_vec: float32 [4, 8, 5, 32, 8, 128], P('win', 'tile')
All inputs are finite; a program needn't handle non-finite values.
Results may differ from a plain program's by a relative error of at most 0.0003.
Values sent between devices are 32-bit elements; how exact they have to be, the bound alone decides.
A program may use at most 64 MiB of HBM per device.

v0:
```python
import functools

import jax
import jax.numpy as jnp
from jax import lax
from jax.experimental import pallas as pl
from jax.experimental.pallas import tpu as pltpu
from jax.sharding import PartitionSpec as P

TY = 4
GROUP = 8

smooth_weight = 0.2


def kernel(windows, tiles, state, obs, winds, coupling, prec, out,
           field, arrived, weighted, later, xs, xr, ys, yr, send, recv, wsend, wrecv):
    variables, levels, cx, cy = state.shape
    steps = winds.shape[0]
    groups = levels // GROUP
    k = lax.axis_index("win")
    t = lax.axis_index("tile")
    before_x, after_x = lax.rem(t + tiles - TY, tiles), lax.rem(t + TY, tiles)
    before_y, after_y = lax.rem(t + tiles - 1, tiles), lax.rem(t + 1, tiles)
    first, last = k == 0, k == windows - 1
    has_next, has_prev = k < windows - 1, k > 0

    barrier = pltpu.get_barrier_semaphore()
    for other in (before_x, after_x, before_y, after_y):
        pl.semaphore_signal(barrier, inc=1, device_id={"tile": other})

    @pl.when(has_next)
    def _():
        pl.semaphore_signal(barrier, inc=1, device_id={"win": k + 1})

    @pl.when(has_prev)
    def _():
        pl.semaphore_signal(barrier, inc=1, device_id={"win": k - 1})

    pl.semaphore_wait(barrier, 4 + has_next.astype(jnp.int32) + has_prev.astype(jnp.int32))

    shape = (GROUP, cx, cy)
    row = lax.broadcasted_iota(jnp.int32, shape, 1)
    lane = lax.broadcasted_iota(jnp.int32, shape, 2)
    level = lax.broadcasted_iota(jnp.int32, shape, 0)

    def copies(slot, g):
        made = []
        for side, (s, r, at, to) in enumerate((
            (xs, xr, 0, before_x), (xs, xr, 1, after_x),
            (ys, yr, 0, before_y), (ys, yr, 1, after_y),
        )):
            made.append(pltpu.make_async_remote_copy(
                src_ref=s.at[slot, at, g], dst_ref=r.at[slot, at, g],
                send_sem=send.at[slot, side, g], recv_sem=recv.at[slot, side, g],
                device_id={"tile": to},
            ))
        return made

    def cut(g):
        return pl.ds(pl.multiple_of(g * GROUP, GROUP), GROUP)

    def onward(g):
        return pltpu.make_async_remote_copy(
            src_ref=field.at[:, cut(g)], dst_ref=arrived.at[:, cut(g)],
            send_sem=wsend.at[0, g], recv_sem=wrecv.at[0, g], device_id={"win": k + 1})

    def back(g):
        return pltpu.make_async_remote_copy(
            src_ref=weighted.at[:, cut(g)], dst_ref=later.at[:, cut(g)],
            send_sem=wsend.at[1, g], recv_sem=wrecv.at[1, g], device_id={"win": k - 1})

    def ship(slot, g, fx, fy):
        low = high = None
        for v in range(variables):
            xs[slot, 0, g, v] = fx[v][:, 0, :]
            xs[slot, 1, g, v] = fx[v][:, cx - 1, :]
            here = lane == level + v * GROUP
            a = jnp.sum(jnp.where(here, fy[v][:, :, :1], 0.0), axis=0)
            b = jnp.sum(jnp.where(here, fy[v][:, :, cy - 1:], 0.0), axis=0)
            low = a if low is None else low + a
            high = b if high is None else high + b
        ys[slot, 0, g] = low
        ys[slot, 1, g] = high
        for copy in copies(slot, g):
            copy.start()

    def receive(slot, g):
        for copy in copies(slot, g):
            copy.wait_recv()

    def beside(slot, g, v, fx, fy):
        here = lane == level + v * GROUP
        north_rim = jnp.sum(jnp.where(here, yr[slot, 0, g][None], 0.0), axis=2, keepdims=True)
        south_rim = jnp.sum(jnp.where(here, yr[slot, 1, g][None], 0.0), axis=2, keepdims=True)
        east = jnp.where(row == cx - 1, xr[slot, 0, g, v][:, None, :], pltpu.roll(fx, cx - 1, 1))
        west = jnp.where(row == 0, xr[slot, 1, g, v][:, None, :], pltpu.roll(fx, 1, 1))
        north = jnp.where(lane == cy - 1, north_rim, pltpu.roll(fy, cy - 1, 2))
        south = jnp.where(lane == 0, south_rim, pltpu.roll(fy, 1, 2))
        return east, west, north, south

    def wind(n, way, g):
        return winds[n, way, cut(g)].astype(jnp.float32)

    def held(ref, g):
        return [ref[v, cut(g)] for v in range(variables)]

    def each(f):
        lax.fori_loop(0, groups, lambda g, c: (f(g), c)[1], 0)

    @pl.when(has_next)
    def _():
        @each
        def _(g):
            f = held(state, g)
            ship(0, g, f, f)

        for n in range(steps):
            @each
            def _(g, n=n):
                receive(n, g)
                f = held(state if n == 0 else field, g)
                u, w = wind(n, 0, g), wind(n, 1, g)
                new = []
                for v in range(variables):
                    e, wst, no, so = beside(n, g, v, f[v], f[v])
                    total = f[v] + u * (e - wst) + w * (no - so)
                    for b in range(variables):
                        total = total + coupling[v, b] * f[b]
                    new.append(total)
                for v in range(variables):
                    field[v, cut(g)] = new[v]
                if n < steps - 1:
                    ship(n + 1, g, new, new)
                else:
                    onward(g).start()

    @pl.when(first)
    def _():
        @each
        def _(g):
            for v in range(variables):
                arrived[v, cut(g)] = jnp.zeros(shape, jnp.float32)

    @each
    def _(g):
        @pl.when(has_prev)
        def _():
            onward(g).wait_recv()
        f = [a - b for a, b in zip(held(state, g), held(arrived, g))]
        ship(steps, g, f, f)

    @each
    def _(g):
        receive(steps, g)
        for v in range(variables):
            f = state[v, cut(g)] - arrived[v, cut(g)]
            e, wst, no, so = beside(steps, g, v, f, f)
            stencil = (1.0 + 4.0 * smooth_weight) * f - smooth_weight * (e + wst + no + so)
            for j in range(GROUP):
                weighted[v, g * GROUP + j] = prec[v, g * GROUP + j] * stencil[j]

        @pl.when(has_prev)
        def _():
            back(g).start()

    @pl.when(has_next)
    def _():
        @each
        def _(g):
            back(g).wait_recv()
            f = held(later, g)
            u, w = wind(steps - 1, 0, g), wind(steps - 1, 1, g)
            ship(steps + 1, g, [u * a for a in f], [w * a for a in f])

        for i in range(steps):
            n = steps - 1 - i
            @each
            def _(g, i=i, n=n):
                slot = steps + 1 + i
                receive(slot, g)
                f = held(later if i == 0 else out, g)
                u, w = wind(n, 0, g), wind(n, 1, g)
                new = []
                for v in range(variables):
                    e, wst, no, so = beside(slot, g, v, u * f[v], w * f[v])
                    total = f[v] + (wst - e) + (so - no)
                    for b in range(variables):
                        total = total + coupling[b, v] * f[b]
                    new.append(total)
                if n > 0:
                    for v in range(variables):
                        out[v, cut(g)] = new[v]
                    u, w = wind(n - 1, 0, g), wind(n - 1, 1, g)
                    ship(slot + 1, g, [u * a for a in new], [w * a for a in new])
                else:
                    for v in range(variables):
                        own = weighted[v, cut(g)] + obs[v, cut(g)] * state[v, cut(g)]
                        out[v, cut(g)] = own - new[v]

    @pl.when(last)
    def _():
        @each
        def _(g):
            for v in range(variables):
                out[v, cut(g)] = weighted[v, cut(g)] + obs[v, cut(g)] * state[v, cut(g)]

    def sent(slot, g):
        for copy in copies(slot, g):
            copy.wait_send()

    @each
    def _(g):
        sent(steps, g)

        @pl.when(has_next)
        def _():
            for i in range(steps):
                sent(i, g)
                sent(steps + 1 + i, g)
            onward(g).wait_send()

        @pl.when(has_prev)
        def _():
            back(g).wait_send()


def solution(mesh):
    windows, tiles = mesh.shape["win"], mesh.shape["tile"]

    def body(state, obs, trajectory, coupling, prec):
        block = state.shape[2:]
        variables, levels, cx, cy = block
        steps = trajectory.shape[2]
        slots, groups = 2 * steps + 1, levels // GROUP
        vmem = pl.BlockSpec(memory_space=pltpu.VMEM)
        smem = pl.BlockSpec(memory_space=pltpu.SMEM)
        f32 = jnp.float32
        result = pl.pallas_call(
            functools.partial(kernel, windows, tiles),
            out_shape=jax.ShapeDtypeStruct(block, f32),
            in_specs=[vmem, vmem, vmem, smem, smem],
            out_specs=vmem,
            scratch_shapes=[pltpu.VMEM(block, f32)] * 4 + [
                pltpu.VMEM((slots, 2, groups, variables, GROUP, cy), f32),
                pltpu.VMEM((slots, 2, groups, variables, GROUP, cy), f32),
                pltpu.VMEM((slots, 2, groups, cx, cy), f32),
                pltpu.VMEM((slots, 2, groups, cx, cy), f32),
                pltpu.SemaphoreType.DMA((slots, 4, groups)),
                pltpu.SemaphoreType.DMA((slots, 4, groups)),
                pltpu.SemaphoreType.DMA((2, groups)),
                pltpu.SemaphoreType.DMA((2, groups)),
            ],
            compiler_params=pltpu.CompilerParams(
                collective_id=0, has_side_effects=True, vmem_limit_bytes=40 * 2**20),
        )(state[0, 0], obs[0, 0], trajectory[0, 0], coupling, prec)
        return result[None, None]

    spec = P("win", "tile", None, None, None, None)
    return jax.shard_map(
        body, mesh=mesh,
        in_specs=(spec, spec, P("win", "tile", None, None, None, None, None), P(), P()),
        out_specs=spec, check_vma=False)
```

profile of v0, /device:TPU:1, one launch (start us, length us, event | category | flops | bytes accessed | tf_op | source)
XLA Modules:
  0.0 72.2 jit_solution(18085996228476186768)
XLA Ops:
  0.0 0.0 copy-start.3
  0.0 0.7 copy-done.3
  0.7 0.0 copy-start
  0.7 1.1 %copy-done = f32[1,1,5,32,8,128]{5,4,3,2,1,0:T(8,128)S(1)} copy-done((f32[1,1,5,32,8,128]{5,4,3,2,1,0:T(8,128)S(1)}, f32[1,1,5,32,8,128]{5,4,3,2,1,0:T(8,128)}, u32[]{:S(2)}) %copy-start) | copy-done | bytes 655384
  1.8 0.0 copy-start.1
  1.8 1.1 %copy-done.1 = f32[1,1,5,32,8,128]{5,4,3,2,1,0:T(8,128)S(1)} copy-done((f32[1,1,5,32,8,128]{5,4,3,2,1,0:T(8,128)S(1)}, f32[1,1,5,32,8,128]{5,4,3,2,1,0:T(8,128)}, u32[]{:S(2)}) %copy-start.1) | copy-done | bytes 655384
  2.9 0.0 copy-start.2
  2.9 1.0 %copy-done.2 = bf16[1,1,3,2,32,8,128]{6,5,4,3,2,1,0:T(8,128)(2,1)S(1)} copy-done((bf16[1,1,3,2,32,8,128]{6,5,4,3,2,1,0:T(8,128)(2,1)S(1)}, bf16[1,1,3,2,32,8,128]{6,5,4,3,2,1,0:T(8,128)(2,1)}, u32[]{:S(2)}) %copy-start.2) | copy-done | bytes 393240
  3.9 0.0 copy-start.4
  3.9 0.7 copy-done.4
  4.5 66.8 %shard_map.55 = f32[5,32,8,128]{3,2,1,0:T(8,128)S(1)} custom-call(f32[5,32,8,128]{3,2,1,0:T(8,128)S(1)} %bitcast.5, f32[5,32,8,128]{3,2,1,0:T(8,128)S(1)} %bitcast.6, bf16[3,2,32,8,128]{4,3,2,1,0:T(8,128)(2,1)S(1)} %bitcast.7, f32[5,5]{1,0:T(8,128)S(1)} %copy-done.3, f32[5,32]{1,0:T(8,128)S(1)} %copy-done.4), custom_call_target="tpu_custom_call" | custom-call | tf_op jit(solution)/shard_map/pallas_call | solution.py:239
  71.3 0.8 %copy.7 = f32[1,1,5,32,8,128]{5,4,3,2,1,0:T(8,128)} copy(f32[1,1,5,32,8,128]{5,4,3,2,1,0:T(8,128)S(1)} %bitcast.4) | data formatting | bytes 1310720
Async XLA Ops:
  0.0 0.7 copy-start.3
  0.7 1.1 %copy-start = (f32[1,1,5,32,8,128]{5,4,3,2,1,0:T(8,128)S(1)}, f32[1,1,5,32,8,128]{5,4,3,2,1,0:T(8,128)}, u32[]{:S(2)}) copy-start(f32[1,1,5,32,8,128]{5,4,3,2,1,0:T(8,128)} %param.5) | copy-start | bytes 1966084
  1.8 1.1 %copy-start.1 = (f32[1,1,5,32,8,128]{5,4,3,2,1,0:T(8,128)S(1)}, f32[1,1,5,32,8,128]{5,4,3,2,1,0:T(8,128)}, u32[]{:S(2)}) copy-start(f32[1,1,5,32,8,128]{5,4,3,2,1,0:T(8,128)} %param.6) | copy-start | bytes 1966084
  2.9 1.0 %copy-start.2 = (bf16[1,1,3,2,32,8,128]{6,5,4,3,2,1,0:T(8,128)(2,1)S(1)}, bf16[1,1,3,2,32,8,128]{6,5,4,3,2,1,0:T(8,128)(2,1)}, u32[]{:S(2)}) copy-start(bf16[1,1,3,2,32,8,128]{6,5,4,3,2,1,0:T(8,128)(2,1)} %param.7) | copy-start | bytes 1179652
  3.9 0.7 copy-start.4
where the time goes:
time: 73.5 us; the launch traced here: 72.2 us
  Pallas kernels  66.8 us (91%)
  local copies, waits for them, and re-layouts  5.38 us (7%)
    pallas_call x1, Pallas kernels, body(): pl.pallas_call(functools.partial(kernel, windows, tiles), out_shape=jax.S...  66.8 us
    unnamed x11, local copies, waits for them, and re-layouts  5.38 us

commit v1 on v0

--- a/solution.py
+++ b/solution.py
@@ -73,8 +73,8 @@
     def ship(slot, g, fx, fy):
         low = high = None
         for v in range(variables):
-            xs[slot, 0, g, v] = fx[v][:, 0, :]
-            xs[slot, 1, g, v] = fx[v][:, cx - 1, :]
+            xs[slot, 0, g, v] = fx[v][:, :1, :]
+            xs[slot, 1, g, v] = fx[v][:, cx - 1:, :]
             here = lane == level + v * GROUP
             a = jnp.sum(jnp.where(here, fy[v][:, :, :1], 0.0), axis=0)
             b = jnp.sum(jnp.where(here, fy[v][:, :, cy - 1:], 0.0), axis=0)
@@ -90,11 +90,12 @@
             copy.wait_recv()
 
     def beside(slot, g, v, fx, fy):
-        here = lane == level + v * GROUP
-        north_rim = jnp.sum(jnp.where(here, yr[slot, 0, g][None], 0.0), axis=2, keepdims=True)
-        south_rim = jnp.sum(jnp.where(here, yr[slot, 1, g][None], 0.0), axis=2, keepdims=True)
-        east = jnp.where(row == cx - 1, xr[slot, 0, g, v][:, None, :], pltpu.roll(fx, cx - 1, 1))
-        west = jnp.where(row == 0, xr[slot, 1, g, v][:, None, :], pltpu.roll(fx, 1, 1))
+        low, high = yr[slot, 0, g], yr[slot, 1, g]
+        spread = [(low[:, p:p + 1], high[:, p:p + 1]) for p in range(v * GROUP, (v + 1) * GROUP)]
+        north_rim = jnp.stack([jnp.broadcast_to(a, shape[1:]) for a, _ in spread])
+        south_rim = jnp.stack([jnp.broadcast_to(b, shape[1:]) for _, b in spread])
+        east = jnp.where(row == cx - 1, xr[slot, 0, g, v], pltpu.roll(fx, cx - 1, 1))
+        west = jnp.where(row == 0, xr[slot, 1, g, v], pltpu.roll(fx, 1, 1))
         north = jnp.where(lane == cy - 1, north_rim, pltpu.roll(fy, cy - 1, 2))
         south = jnp.where(lane == 0, south_rim, pltpu.roll(fy, 1, 2))
         return east, west, north, south
@@ -135,6 +136,8 @@
                 else:
                     onward(g).start()
 
+    own_rims = jnp.where(first, 0, steps)
+
     @pl.when(first)
     def _():
         @each
@@ -147,15 +150,17 @@
         @pl.when(has_prev)
         def _():
             onward(g).wait_recv()
-        f = [a - b for a, b in zip(held(state, g), held(arrived, g))]
-        ship(steps, g, f, f)
+            f = [a - b for a, b in zip(held(state, g), held(arrived, g))]
+            ship(steps, g, f, f)
 
     @each
     def _(g):
-        receive(steps, g)
+        @pl.when(has_prev)
+        def _():
+            receive(steps, g)
         for v in range(variables):
             f = state[v, cut(g)] - arrived[v, cut(g)]
-            e, wst, no, so = beside(steps, g, v, f, f)
+            e, wst, no, so = beside(own_rims, g, v, f, f)
             stencil = (1.0 + 4.0 * smooth_weight) * f - smooth_weight * (e + wst + no + so)
             for j in range(GROUP):
                 weighted[v, g * GROUP + j] = prec[v, g * GROUP + j] * stencil[j]
@@ -211,8 +216,6 @@
 
     @each
     def _(g):
-        sent(steps, g)
-
         @pl.when(has_next)
         def _():
             for i in range(steps):
@@ -223,6 +226,7 @@
         @pl.when(has_prev)
         def _():
             back(g).wait_send()
+            sent(steps, g)
 
 
 def solution(mesh):
@@ -242,8 +246,8 @@
             in_specs=[vmem, vmem, vmem, smem, smem],
             out_specs=vmem,
             scratch_shapes=[pltpu.VMEM(block, f32)] * 4 + [
-                pltpu.VMEM((slots, 2, groups, variables, GROUP, cy), f32),
-                pltpu.VMEM((slots, 2, groups, variables, GROUP, cy), f32),
+                pltpu.VMEM((slots, 2, groups, variables, GROUP, 1, cy), f32),
+                pltpu.VMEM((slots, 2, groups, variables, GROUP, 1, cy), f32),
                 pltpu.VMEM((slots, 2, groups, cx, cy), f32),
                 pltpu.VMEM((slots, 2, groups, cx, cy), f32),
                 pltpu.SemaphoreType.DMA((slots, 4, groups)),

time: 73.5 us -> 68.7 us (0.935); the launches traced: 72.2 us -> 68.4 us
  Pallas kernels: 66.8 us -> 63 us
    pallas_call x1, Pallas kernels: 66.8 us -> 63 us  [body(): pl.pallas_call(functools.partial(kernel, windows, tiles), out_shape=jax.S...]
where the time goes in v1:
time: 68.7 us; the launch traced here: 68.4 us
  Pallas kernels  63 us (92%)
  local copies, waits for them, and re-layouts  5.38 us (8%)
    pallas_call x1, Pallas kernels, body(): pl.pallas_call(functools.partial(kernel, windows, tiles), out_shape=jax.S...  63 us
    unnamed x11, local copies, waits for them, and re-layouts  5.38 us

profile of v1, /device:TPU:1, one launch (start us, length us, event | category | flops | bytes accessed | tf_op | source)
XLA Modules:
  0.0 68.4 jit_solution(16648908211135682953)
XLA Ops:
  0.0 0.0 copy-start.3
  0.0 0.7 %copy-done.3 = f32[5,5]{1,0:T(8,128)S(1)} copy-done((f32[5,5]{1,0:T(8,128)S(1)}, f32[5,5]{1,0:T(8,128)}, u32[]{:S(2)}) %copy-start.3) | copy-done | bytes 124
  0.7 0.0 copy-start
  0.7 1.1 %copy-done = f32[1,1,5,32,8,128]{5,4,3,2,1,0:T(8,128)S(1)} copy-done((f32[1,1,5,32,8,128]{5,4,3,2,1,0:T(8,128)S(1)}, f32[1,1,5,32,8,128]{5,4,3,2,1,0:T(8,128)}, u32[]{:S(2)}) %copy-start) | copy-done | bytes 655384
  1.8 0.0 copy-start.1
  1.8 1.1 %copy-done.1 = f32[1,1,5,32,8,128]{5,4,3,2,1,0:T(8,128)S(1)} copy-done((f32[1,1,5,32,8,128]{5,4,3,2,1,0:T(8,128)S(1)}, f32[1,1,5,32,8,128]{5,4,3,2,1,0:T(8,128)}, u32[]{:S(2)}) %copy-start.1) | copy-done | bytes 655384
  2.9 0.0 copy-start.2
  2.9 1.0 %copy-done.2 = bf16[1,1,3,2,32,8,128]{6,5,4,3,2,1,0:T(8,128)(2,1)S(1)} copy-done((bf16[1,1,3,2,32,8,128]{6,5,4,3,2,1,0:T(8,128)(2,1)S(1)}, bf16[1,1,3,2,32,8,128]{6,5,4,3,2,1,0:T(8,128)(2,1)}, u32[]{:S(2)}) %copy-start.2) | copy-done | bytes 393240
  3.9 0.0 copy-start.4
  3.9 0.7 %copy-done.4 = f32[5,32]{1,0:T(8,128)S(1)} copy-done((f32[5,32]{1,0:T(8,128)S(1)}, f32[5,32]{1,0:T(8,128)}, u32[]{:S(2)}) %copy-start.4) | copy-done | bytes 664
  4.5 63.0 %shard_map.55 = f32[5,32,8,128]{3,2,1,0:T(8,128)S(1)} custom-call(f32[5,32,8,128]{3,2,1,0:T(8,128)S(1)} %bitcast.5, f32[5,32,8,128]{3,2,1,0:T(8,128)S(1)} %bitcast.6, bf16[3,2,32,8,128]{4,3,2,1,0:T(8,128)(2,1)S(1)} %bitcast.7, f32[5,5]{1,0:T(8,128)S(1)} %copy-done.3, f32[5,32]{1,0:T(8,128)S(1)} %copy-done.4), custom_call_target="tpu_custom_call" | custom-call | tf_op jit(solution)/shard_map/pallas_call | solution.py:243
  67.6 0.8 %copy.7 = f32[1,1,5,32,8,128]{5,4,3,2,1,0:T(8,128)} copy(f32[1,1,5,32,8,128]{5,4,3,2,1,0:T(8,128)S(1)} %bitcast.4) | data formatting | bytes 1310720
Async XLA Ops:
  0.0 0.7 %copy-start.3 = (f32[5,5]{1,0:T(8,128)S(1)}, f32[5,5]{1,0:T(8,128)}, u32[]{:S(2)}) copy-start(f32[5,5]{1,0:T(8,128)} %coupling.1) | copy-start | bytes 304
  0.7 1.1 %copy-start = (f32[1,1,5,32,8,128]{5,4,3,2,1,0:T(8,128)S(1)}, f32[1,1,5,32,8,128]{5,4,3,2,1,0:T(8,128)}, u32[]{:S(2)}) copy-start(f32[1,1,5,32,8,128]{5,4,3,2,1,0:T(8,128)} %param.5) | copy-start | bytes 1966084
  1.8 1.1 %copy-start.1 = (f32[1,1,5,32,8,128]{5,4,3,2,1,0:T(8,128)S(1)}, f32[1,1,5,32,8,128]{5,4,3,2,1,0:T(8,128)}, u32[]{:S(2)}) copy-start(f32[1,1,5,32,8,128]{5,4,3,2,1,0:T(8,128)} %param.6) | copy-start | bytes 1966084
  2.9 1.0 %copy-start.2 = (bf16[1,1,3,2,32,8,128]{6,5,4,3,2,1,0:T(8,128)(2,1)S(1)}, bf16[1,1,3,2,32,8,128]{6,5,4,3,2,1,0:T(8,128)(2,1)}, u32[]{:S(2)}) copy-start(bf16[1,1,3,2,32,8,128]{6,5,4,3,2,1,0:T(8,128)(2,1)} %param.7) | copy-start | bytes 1179652
  3.9 0.7 %copy-start.4 = (f32[5,32]{1,0:T(8,128)S(1)}, f32[5,32]{1,0:T(8,128)}, u32[]{:S(2)}) copy-start(f32[5,32]{1,0:T(8,128)} %prec.1) | copy-start | bytes 1924
